TPU v7x, 16 devices: a 4x2x1 block of a 4x4x8 slice. The times are simulated.
16 devices in a mesh: dp: 2 (over y, z), tp: 8 (over x, core).
Axes of the slice: x: 4, y: 2, z: 1, core: 2. Of those that a mesh axis runs over, the one named last changes fastest.
The devices are a block of a 4x4x8 slice.
Arguments:
- hidden: bfloat16 [512, 1152], P('dp', 'tp'), parts along dimension 0
- cand_ids: int32 [512, 4], P('dp'), parts along dimension 0
- norm_scale: bfloat16 [1152], P('tp')
- emb_table: bfloat16 [262144, 1152], P('tp')
Outputs:
- output 1: float32 [512], P('dp'), parts along dimension 0
- output 2: float32 [512, 4], P('dp'), parts along dimension 0
- output 3: bfloat16 [512, 262144], P('dp', 'tp'), parts along dimension 0
There are 2 independent parts. A program takes and returns all parts, laid end to end along the dimension named above; an argument that names none is the same for every part.
All inputs are finite; a program needn't handle non-finite values.
Results may differ from a plain program's by a relative error of at most 0.001.
Values are sent between devices in bfloat16 or wider.
A program may use at most 768 MiB of HBM per device.

v0:
```python
import jax
import jax.numpy as jnp
from jax import lax
from jax.sharding import PartitionSpec as P

NORM_EPS = 1e-6
SOFT_CAP = 30.0


def solution(mesh):
    group_size = mesh.shape["tp"]

    def device_step(hidden_blk, cand_ids, scale_blk, table_blk):
        hidden_f32 = hidden_blk.astype(jnp.float32)
        full_width = hidden_blk.shape[1] * group_size
        sq_sum = lax.psum(jnp.sum(hidden_f32 * hidden_f32, axis=1, keepdims=True), "tp")
        normed = (hidden_f32 * lax.rsqrt(sq_sum / full_width + NORM_EPS) * (1.0 + scale_blk.astype(jnp.float32))).astype(jnp.bfloat16)
        full_normed = lax.all_gather(normed, "tp", axis=1, tiled=True)
        logits = lax.dot_general(full_normed, table_blk, (((1,), (1,)), ((), ())), preferred_element_type=jnp.float32)
        capped = SOFT_CAP * jnp.tanh(logits / SOFT_CAP)
        local_max = jnp.max(capped, axis=1)
        local_sum = jnp.sum(jnp.exp(capped - local_max[:, None]), axis=1)
        shard_stats = lax.all_gather(jnp.stack([local_max, local_sum]), "tp")
        glob_max = jnp.max(shard_stats[:, 0], axis=0)
        glob_sum = jnp.sum(shard_stats[:, 1] * jnp.exp(shard_stats[:, 0] - glob_max[None, :]), axis=0)
        row_lse = glob_max + jnp.log(glob_sum)
        log_probs = capped - row_lse[:, None]
        vocab_local = table_blk.shape[0]
        local_ids = cand_ids - lax.axis_index("tp") * vocab_local
        is_owned = (local_ids >= 0) & (local_ids < vocab_local)
        picked = jnp.take_along_axis(capped, jnp.clip(local_ids, 0, vocab_local - 1), axis=1)
        cand_capped = lax.psum(jnp.where(is_owned, picked, 0.0), "tp")
        return row_lse, cand_capped - row_lse[:, None], log_probs.astype(jnp.bfloat16)

    return jax.shard_map(
        device_step,
        mesh=mesh,
        in_specs=(P("dp", "tp"), P("dp", None), P("tp"), P("tp", None)),
        out_specs=(P("dp"), P("dp", None), P("dp", "tp")),
        check_vma=False,
    )
```

profile of v0, /device:TPU:113, one launch (start us, length us, event | category | flops | bytes accessed | tf_op | source)
XLA Modules:
  0.0 172.9 jit_solution(13479369722026515559)
XLA Ops:
  0.6 0.7 convert_add_fusion
  1.3 0.9 fusion.2
  2.2 13.6 %psum.14 = f32[256,1]{0,1:T(1,128)S(1)} all-reduce(f32[256,1]{0,1:T(1,128)S(1)} %bitcast.25), channel_id=1, replica_groups=mesh['dp'=2,'tp'=8] {'tp'}, use_global_device_ids=true, to_apply=%region_1.0 | all-reduce | flops 256 | bytes 2048 | tf_op jit(solution)/shard_map/psum | solution.py:16
  15.8 1.0 fusion.4
  16.8 19.0 %all_gather.9 = bf16[256,1152]{0,1:T(8,128)(2,1)S(1)} all-gather(bf16[256,144]{0,1:T(8,128)(2,1)S(1)} %fusion.4), channel_id=1, replica_groups=mesh['dp'=2,'tp'=8] {'tp'}, dimensions={1}, use_global_device_ids=true | all-gather | bytes 663552 | tf_op jit(solution)/shard_map/all_gather | solution.py:18
  35.8 40.9 %fusion.9 = (f32[256]{0:T(256)S(1)}, f32[256,32768]{1,0:T(8,128)}) fusion(bf16[256,1152]{0,1:T(8,128)(2,1)S(1)} %all_gather.9, bf16[32768,1152]{1,0:T(8,128)(2,1)} %param.7), kind=kOutput, calls=%fused_computation.26 | convolution fusion | flops 19352518656 | bytes 109642752 | tf_op jit(solution)/shard_map/dot_general | solution.py:19
  76.7 0.0 copy-start
  76.7 13.7 %exponential_reduce_fusion = f32[256]{0:T(256)S(1)} fusion(f32[256,32768]{1,0:T(8,128)} %get-tuple-element.13, f32[256]{0:T(256)S(1)} %get-tuple-element.12), kind=kLoop, calls=%fused_computation.5 | loop fusion | flops 16776960 | bytes 33556480 | tf_op jit(solution)/shard_map/reduce_sum | solution.py:22
  90.3 22.4 %all-gather.1 = f32[8,2,256]{2,1,0:T(2,128)S(1)} all-gather(f32[1,2,256]{2,1,0:T(2,128)S(1)} %maximum_bitcast_fusion), channel_id=2, replica_groups=mesh['dp'=2,'tp'=8] {'tp'}, dimensions={0}, use_global_device_ids=true | all-gather | bytes 18432 | tf_op jit(solution)/shard_map/all_gather | solution.py:23
  112.8 0.0 copy-start.1
  112.8 0.0 copy-done
  112.9 0.1 copy.25
  113.0 0.1 reshape.25
  113.1 21.1 %gather_fusion = f32[1024]{0:T(1024)S(1)} fusion(f32[256,32768]{1,0:T(8,128)} %get-tuple-element.13, s32[1024]{0:T(1024)S(1)} %reshape.25), kind=kCustom, calls=%fused_computation | custom fusion | bytes 16384 | tf_op jit(solution)/shard_map/jit(take_along_axis)/gather | solution.py:31
  134.3 0.1 reshape.28
  134.4 0.1 copy.26
  134.5 20.3 %psum.15 = f32[256,4]{0,1:T(4,128)S(1)} all-reduce(f32[256,4]{0,1:T(4,128)S(1)} %select_select_fusion), channel_id=1, replica_groups=mesh['dp'=2,'tp'=8] {'tp'}, use_global_device_ids=true, to_apply=%region_6.7 | all-reduce | flops 1024 | bytes 8192 | tf_op jit(solution)/shard_map/psum | solution.py:32
  154.8 0.6 broadcast_subtract_fusion
  155.4 0.0 copy-done.1
  155.4 17.5 %subtract_convert_fusion = bf16[256,32768]{1,0:T(8,128)(2,1)} fusion(f32[256,32768]{1,0:T(8,128)} %get-tuple-element.13, f32[256]{0:T(256)S(1)} %log_add_fusion), kind=kLoop, calls=%fused_computation.4 | loop fusion | flops 16777216 | bytes 50332672 | tf_op jit(solution)/shard_map/convert_element_type | solution.py:33
  (7 shorter events, 0.1 us)
Async XLA Ops:
  76.7 36.2 %copy-start = (s32[256,4]{0,1:T(4,128)S(1)}, s32[256,4]{0,1:T(4,128)}, u32[]{:S(2)}) copy-start(s32[256,4]{0,1:T(4,128)} %param.5) | copy-start | bytes 12292
  112.8 42.6 %copy-start.1 = (f32[256]{0:T(256)}, f32[256]{0:T(256)S(1)}, u32[]{:S(2)}) copy-start(f32[256]{0:T(256)S(1)} %log_add_fusion) | copy-start | bytes 3076
where the time goes:
time: 174 us; the launch traced here: 173 us
  blocking collectives  75.3 us (43%)
  matrix products  40.9 us (24%)
  other arithmetic  34.4 us (20%)
  local copies, waits for them, and re-layouts  21.6 us (12%)
    dot_general x1, matrix products, device_step(): lax.dot_general(full_normed, table_blk, (((1,), (1,)), ((), ())), preferr...  40.9 us
    all_gather x1, blocking collectives, device_step(): shard_stats = lax.all_gather(jnp.stack([local_max, local_sum]), 'tp')  22.4 us
    gather x5, local copies, waits for them, and re-layouts, device_step(): jnp.take_along_axis(capped, jnp.clip(local_ids, 0, vocab_local - 1), axis=1)  21.6 us
    psum x1, blocking collectives, device_step(): cand_capped = lax.psum(jnp.where(is_owned, picked, 0.0), 'tp')  20.3 us
    all_gather x1, blocking collectives, device_step(): full_normed = lax.all_gather(normed, 'tp', axis=1, tiled=True)  19 us
    convert_element_type x1, other arithmetic, device_step(): log_probs.astype(jnp.bfloat16)  17.5 us
    reduce_sum x1, other arithmetic, device_step(): local_sum = jnp.sum(jnp.exp(capped - local_max[:, None]), axis=1)  13.7 us
    psum x1, blocking collectives, device_step(): lax.psum(jnp.sum(hidden_f32 * hidden_f32, axis=1, keepdims=True), 'tp')  13.6 us

commit v1 on v0

v1 whole, which is shorter than its diff:
```python
import functools
import math

import jax
import jax.numpy as jnp
from jax import lax
from jax.experimental import pallas as pl
from jax.experimental.pallas import tpu as pltpu
from jax.sharding import PartitionSpec as P

NORM_EPS = 1e-6
SOFT_CAP = 30.0
LOG2E = math.log2(math.e)
CHUNK = 1024
RING = 10
OUT_ROWS = 16
OUT_RING = 4
MESH = pl.DeviceIdType.MESH


def head_kernel(n, h_hbm, s_hbm, ids_ref, tab_hbm, c_ref, tail_ref,
                ebuf, gath, s_all, s_col, normed, z_a, z_b, stats,
                e_sem, in_sem, s_sem, s_recv, own_send, own_recv, far_send, far_recv,
                relay_send, relay_recv, st_send, st_recv):
    me = lax.axis_index("tp")
    core = lax.rem(me, 2)
    mate = me + 1 - 2 * core
    chips = n // 2
    vocab, width = tab_hbm.shape
    rows = normed.shape[1]
    feat = h_hbm.shape[0]
    n_chunks = vocab // CHUNK

    def far(d):
        return lax.rem(me + 2 * d, n)

    def from_far(d):
        return lax.rem(me + n - 2 * d, n)

    def table_copy(j):
        slot = lax.rem(j, RING)
        return pltpu.make_async_copy(
            tab_hbm.at[pl.ds(pl.multiple_of(j * CHUNK, CHUNK), CHUNK), :],
            ebuf.at[slot], e_sem.at[slot])

    def remote(src, dst, send, recv, peer):
        return pltpu.make_async_remote_copy(
            src_ref=src, dst_ref=dst, send_sem=send, recv_sem=recv,
            device_id={"tp": peer}, device_id_type=MESH)

    h_in = pltpu.make_async_copy(h_hbm, gath.at[me], in_sem.at[0])
    s_in = pltpu.make_async_copy(s_hbm, s_all.at[me], in_sem.at[1])
    h_in.start()
    s_in.start()
    barrier = pltpu.get_barrier_semaphore()
    for d in range(1, n):
        pl.semaphore_signal(barrier, inc=1, device_id={"tp": lax.rem(me + d, n)}, device_id_type=MESH)
    for j in range(RING):
        table_copy(j).start()
    s_in.wait()
    h_in.wait()
    pl.semaphore_wait(barrier, n - 1)

    far_copies = [remote(gath.at[me], gath.at[me], far_send.at[d - 1], far_recv.at[d - 1], far(d)) for d in range(1, chips)]
    own_copy = remote(gath.at[me], gath.at[me], own_send, own_recv, mate)
    s_copies = [remote(s_all.at[me], s_all.at[me], s_sem.at[d - 1], s_recv.at[d - 1], lax.rem(me + d, n)) for d in range(1, n)]
    for cp in s_copies:
        cp.start()
    for cp in far_copies:
        cp.start()
    own_copy.start()

    for cp in s_copies:
        cp.wait()
    for d in range(n):
        s_row = 1.0 + s_all[d].astype(jnp.float32)
        pad = jnp.zeros((1, 256 - feat), jnp.float32)
        s_wide = jnp.broadcast_to(jnp.concatenate([s_row, pad], axis=1), (128, 256))
        s_col[d * feat:(d + 1) * feat, :] = s_wide.T[:feat, :]

    relays = []
    order = sorted(range(1, chips), key=lambda d: min(d, chips - d))
    for d in order:
        far_copies[d - 1].wait_recv()
        src = from_far(d)
        cp = remote(gath.at[src], gath.at[src], relay_send.at[d - 1], relay_recv.at[d - 1], mate)
        cp.start()
        relays.append(cp)
    own_copy.wait()
    for cp in relays:
        cp.wait_recv()

    sq = jnp.zeros((8, rows), jnp.float32)
    for d in range(n):
        h32 = gath[d].astype(jnp.float32)
        sq = sq + jnp.sum((h32 * h32).reshape(feat // 8, 8, rows), axis=0)
    mean_sq = jnp.sum(sq, axis=0, keepdims=True) / width
    inv = lax.rsqrt(mean_sq + NORM_EPS)
    for d in range(n):
        scale = s_col[d * feat:(d + 1) * feat, :]
        scale = jnp.concatenate([scale] * (rows // 128), axis=1)
        normed[d * feat:(d + 1) * feat, :] = (gath[d].astype(jnp.float32) * inv * scale).astype(jnp.bfloat16)
    for cp in far_copies:
        cp.wait_send()
    for cp in relays:
        cp.wait_send()

    def multiply(j, z_ref):
        z_ref[...] = jnp.dot(ebuf[lax.rem(j, RING)], normed[...], preferred_element_type=jnp.float32)

    n_cand = ids_ref.shape[0]
    first = me * vocab
    sub = lax.broadcasted_iota(jnp.int32, (8, rows), 0)

    def finish(j, z_ref, carry):
        acc, picks = carry[0], list(carry[1:])
        want = [ids_ref[k:k + 1, :] - (first + j * CHUNK) - sub for k in range(n_cand)]
        for b in range(CHUNK // 128):
            x = z_ref[b * 128:(b + 1) * 128, :]
            t = jnp.tanh(x * (1.0 / SOFT_CAP))
            e = jnp.exp2(t * (SOFT_CAP * LOG2E))
            acc = acc + jnp.sum(e.reshape(16, 8, rows), axis=0)
            c = t * SOFT_CAP
            for g in range(16):
                part = c[g * 8:(g + 1) * 8, :]
                for k in range(n_cand):
                    picks[k] = jnp.where(want[k] == b * 128 + g * 8, part, picks[k])
            c_ref[:, pl.ds(pl.multiple_of(j * CHUNK + b * 128, 128), 128)] = c.T
        return (acc, *picks)

    table_copy(0).wait()
    multiply(0, z_a)

    def pair(p, acc):
        a = 2 * p
        for k in (1, 2):
            table_copy(a + k).wait()
        for k in (-1, 0):
            nxt = a + k + RING

            @pl.when((nxt >= RING) & (nxt < n_chunks))
            def _():
                table_copy(nxt).start()
        multiply(a + 1, z_b)
        acc = finish(a, z_a, acc)
        multiply(a + 2, z_a)
        return finish(a + 1, z_b, acc)

    acc = lax.fori_loop(0, n_chunks // 2 - 1, pair, (jnp.zeros((8, rows), jnp.float32),) * (1 + n_cand))
    table_copy(n_chunks - 1).wait()
    multiply(n_chunks - 1, z_b)
    acc = finish(n_chunks - 2, z_a, acc)
    acc = finish(n_chunks - 1, z_b, acc)

    for k, part in enumerate(acc):
        stats[me, k:k + 1, :] = jnp.sum(part, axis=0, keepdims=True)
    st_copies = [remote(stats.at[me], stats.at[me], st_send.at[d - 1], st_recv.at[d - 1], lax.rem(me + d, n)) for d in range(1, n)]
    for cp in st_copies:
        cp.start()
    for cp in st_copies:
        cp.wait()
    total = stats[0]
    for d in range(1, n):
        total = total + stats[d]
    lse = jnp.log(total[0:1, :])
    tail_ref[0:1, :] = lse
    tail_ref[1:1 + n_cand, :] = total[1:1 + n_cand, :] - lse


def write_kernel(c_ref, tail_ref, lse_ref, cand_ref, out_hbm, l_col, obuf, o_sem):
    rows, vocab = c_ref.shape
    lse_ref[...] = tail_ref[0:1, :]
    cand_ref[...] = tail_ref[1:1 + cand_ref.shape[0], :]
    for b in range(rows // 128):
        l_col[b * 128:(b + 1) * 128, :] = jnp.broadcast_to(tail_ref[0:1, b * 128:(b + 1) * 128], (128, 128)).T
    n_blk = rows // OUT_ROWS

    def out_copy(i, slot):
        return pltpu.make_async_copy(
            obuf.at[slot], out_hbm.at[pl.ds(pl.multiple_of(i * OUT_ROWS, OUT_ROWS), OUT_ROWS), :], o_sem.at[slot])

    def block(i, carry):
        slot = lax.rem(i, OUT_RING)

        @pl.when(i >= OUT_RING)
        def _():
            out_copy(i - OUT_RING, slot).wait()
        r0 = pl.multiple_of(i * OUT_ROWS, OUT_ROWS)
        col = l_col[pl.ds(r0, OUT_ROWS), :]
        step = 2048

        def part(q, c):
            v0 = pl.multiple_of(q * step, step)
            lse = jnp.concatenate([col] * (step // 128), axis=1)
            obuf[slot, :, pl.ds(v0, step)] = (c_ref[pl.ds(r0, OUT_ROWS), pl.ds(v0, step)] - lse).astype(jnp.bfloat16)
            return c

        lax.fori_loop(0, vocab // step, part, 0)
        out_copy(i, slot).start()
        return carry

    lax.fori_loop(0, n_blk, block, 0)
    for i in range(n_blk - OUT_RING, n_blk):
        out_copy(i, i % OUT_RING).wait()


def solution(mesh):
    n = mesh.shape["tp"]

    def device_step(hidden_blk, cand_ids, scale_blk, table_blk):
        rows, feat = hidden_blk.shape
        vocab, width = table_blk.shape
        n_cand = cand_ids.shape[1]
        ids_t = cand_ids.T
        dma = pltpu.SemaphoreType.DMA
        any_space = pl.BlockSpec(memory_space=pl.ANY)
        vmem = pl.BlockSpec(memory_space=pltpu.VMEM)
        capped, tail = pl.pallas_call(
            functools.partial(head_kernel, n),
            out_shape=(pltpu.VMEM((rows, vocab), jnp.float32),
                       jax.ShapeDtypeStruct((8, rows), jnp.float32)),
            in_specs=[any_space, any_space, vmem, any_space],
            out_specs=(vmem, vmem),
            scratch_shapes=[
                pltpu.VMEM((RING, CHUNK, width), jnp.bfloat16),
                pltpu.VMEM((n, feat, rows), jnp.bfloat16),
                pltpu.VMEM((n, 1, feat), jnp.bfloat16),
                pltpu.VMEM((n * feat, 128), jnp.float32),
                pltpu.VMEM((n * feat, rows), jnp.bfloat16),
                pltpu.VMEM((CHUNK, rows), jnp.float32),
                pltpu.VMEM((CHUNK, rows), jnp.float32),
                pltpu.VMEM((n, 8, rows), jnp.float32),
                dma((RING,)), dma((2,)), dma((n - 1,)), dma((n - 1,)), dma, dma,
                dma((n // 2 - 1,)), dma((n // 2 - 1,)), dma((n // 2 - 1,)), dma((n // 2 - 1,)),
                dma((n - 1,)), dma((n - 1,)),
            ],
            compiler_params=pltpu.CompilerParams(
                collective_id=0, has_side_effects=True, vmem_limit_bytes=31 * 2**20),
        )(hidden_blk.T, scale_blk.reshape(1, feat), ids_t, table_blk)
        lse, cand, logp = pl.pallas_call(
            write_kernel,
            out_shape=(jax.ShapeDtypeStruct((1, rows), jnp.float32),
                       jax.ShapeDtypeStruct((n_cand, rows), jnp.float32),
                       jax.ShapeDtypeStruct((rows, vocab), jnp.bfloat16)),
            in_specs=[vmem, vmem],
            out_specs=(vmem, vmem, any_space),
            scratch_shapes=[pltpu.VMEM((rows, 128), jnp.float32),
                            pltpu.VMEM((OUT_RING, OUT_ROWS, vocab), jnp.bfloat16),
                            dma((OUT_RING,))],
            compiler_params=pltpu.CompilerParams(vmem_limit_bytes=31 * 2**20),
        )(pltpu.with_memory_space_constraint(capped, pltpu.VMEM), tail)
        return lse.reshape(rows), cand.T, logp

    return jax.shard_map(
        device_step,
        mesh=mesh,
        in_specs=(P("dp", "tp"), P("dp", None), P("tp"), P("tp", None)),
        out_specs=(P("dp"), P("dp", None), P("dp", "tp")),
        check_vma=False,
    )
```

time: 174 us -> 58.6 us (0.34)
  blocking collectives: 75.3 us -> 0 us
  Pallas kernels: 0 us -> 56.6 us
  matrix products: 40.9 us -> 0 us
  other arithmetic: 34.4 us -> 0 us
  local copies, waits for them, and re-layouts: 21.6 us -> 1.22 us
    pallas_call x0 -> x2, Pallas kernels: none -> 56.6 us  [the longest x1 49.1 us: device_step(): pl.pallas_call(functools.partial(head_kernel, n), out_shape=(pltpu.VMEM((...]
    all_gather x2 -> x0, blocking collectives: 41.4 us -> none  [the longest x1 22.4 us: device_step(): shard_stats = lax.all_gather(jnp.stack([local_max, local_sum]), 'tp')]
    dot_general x1 -> x0, matrix products: 40.9 us -> none  [device_step(): lax.dot_general(full_normed, table_blk, (((1,), (1,)), ((), ())), preferr...]
    psum x2 -> x0, blocking collectives: 33.9 us -> none  [the longest x1 20.3 us: device_step(): cand_capped = lax.psum(jnp.where(is_owned, picked, 0.0), 'tp')]
    gather x5 -> x0, local copies, waits for them, and re-layouts: 21.6 us -> none  [device_step(): jnp.take_along_axis(capped, jnp.clip(local_ids, 0, vocab_local - 1), axis=1)]
    convert_element_type x2 -> x0, other arithmetic: 18.4 us -> none  [the longest x1 17.5 us: device_step(): log_probs.astype(jnp.bfloat16)]
    reduce_sum x3 -> x0, other arithmetic: 14.6 us -> none  [the longest x1 13.7 us: device_step(): local_sum = jnp.sum(jnp.exp(capped - local_max[:, None]), axis=1)]
where the time goes in v1:
time: 58.6 us; the launch traced here: 58.4 us
  Pallas kernels  56.6 us (97%)
  local copies, waits for them, and re-layouts  1.22 us (2%)
  between operations  0.64 us (1%)
    pallas_call x1, Pallas kernels, device_step(): pl.pallas_call(functools.partial(head_kernel, n), out_shape=(pltpu.VMEM((...  49.1 us
    pallas_call x1, Pallas kernels, device_step(): pl.pallas_call(write_kernel, out_shape=(jax.ShapeDtypeStruct((1, rows), j...  7.46 us
    reshape x1, local copies, waits for them, and re-layouts, device_step(): scale_blk.reshape(1, feat)  1.22 us

profile of v1, /device:TPU:113, one launch (start us, length us, event | category | flops | bytes accessed | tf_op | source)
XLA Modules:
  0.0 58.4 jit_solution(5813846880435107203)
XLA Ops:
  0.6 1.2 %reshape.12.s_hbm = bf16[1,144]{1,0:T(2,128)(2,1)} reshape(bf16[144]{0:T(256)(128)(2,1)} %param.6) | data formatting | bytes 576 | tf_op jit(solution)/shard_map/reshape | solution.py:239
  1.9 49.1 %shard_map.67 = (f32[256,32768]{1,0:T(8,128)S(1)}, f32[8,256]{1,0:T(8,128)}) custom-call(bf16[144,256]{1,0:T(8,128)(2,1)} %bitcast.4, bf16[1,144]{1,0:T(2,128)(2,1)} %reshape.12.s_hbm, s32[4,256]{1,0:T(4,128)} %bitcast.5, bf16[32768,1152]{1,0:T(8,128)(2,1)} %tab_hbm.1), custom_call_target="tpu_custom_call" | custom-call | tf_op jit(solution)/shard_map/pallas_call | solution.py:218
  51.0 7.5 %shard_map.68 = (f32[1,256]{1,0:T(1,128)}, f32[4,256]{1,0:T(4,128)}, bf16[256,32768]{1,0:T(8,128)(2,1)}) custom-call(f32[256,32768]{1,0:T(8,128)S(1)} %get-tuple-element.8.c_ref, f32[8,256]{1,0:T(8,128)} %get-tuple-element.9.tail_ref), custom_call_target="tpu_custom_call" | custom-call | tf_op jit(solution)/shard_map/pallas_call | solution.py:240

commit v2 on v1

v2 whole, which is shorter than its diff:
```python
import functools
import math

import jax
import jax.numpy as jnp
from jax import lax
from jax.experimental import pallas as pl
from jax.experimental.pallas import tpu as pltpu
from jax.sharding import PartitionSpec as P

NORM_EPS = 1e-6
SOFT_CAP = 30.0
LOG2E = math.log2(math.e)
CHUNK = 1024
RING = 10
OUT_ROWS = 16
OUT_RING = 4
MESH = pl.DeviceIdType.MESH


def head_kernel(n, h_hbm, s_hbm, ids_hbm, tab_hbm, c_ref, tail_ref,
                ebuf, gath, s_own, s_all, s_col, sq_part, normed, z_a, z_b, ids_ref, stats,
                e_sem, in_sem, s_send, s_recv, h_send, h_recv, mate_send, mate_recv, st_send, st_recv):
    me = lax.axis_index("tp")
    core = lax.rem(me, 2)
    mate = me + 1 - 2 * core
    vocab, width = tab_hbm.shape
    feat, rows = h_hbm.shape
    halves = gath.shape[1]
    n_chunks = vocab // CHUNK
    n_cand = ids_hbm.shape[0]

    onward = lax.rem(me + 2 + core * (n - 4), n)
    behind = lax.rem(me + n - 2 - core * (n - 4), n)
    across = lax.rem(me + 4, n)

    def table_copy(j):
        slot = lax.rem(j, RING)
        return pltpu.make_async_copy(
            tab_hbm.at[pl.ds(pl.multiple_of(j * CHUNK, CHUNK), CHUNK), :],
            ebuf.at[slot], e_sem.at[slot])

    def remote(ref, send, recv, peer):
        return pltpu.make_async_remote_copy(
            src_ref=ref, dst_ref=ref, send_sem=send, recv_sem=recv,
            device_id={"tp": peer}, device_id_type=MESH)

    h_in = [pltpu.make_async_copy(h_hbm.at[:, pl.ds(q * 128, 128)], gath.at[me, q], in_sem.at[q]) for q in range(halves)]
    s_in = pltpu.make_async_copy(s_hbm, s_own, in_sem.at[halves])
    i_in = pltpu.make_async_copy(ids_hbm, ids_ref, in_sem.at[halves + 1])
    for cp in h_in + [s_in, i_in]:
        cp.start()
    barrier = pltpu.get_barrier_semaphore()
    for d in range(1, n):
        pl.semaphore_signal(barrier, inc=1, device_id={"tp": lax.rem(me + d, n)}, device_id_type=MESH)
    for j in range(RING):
        table_copy(j).start()
    s_in.wait()
    s_all[me] = s_own[...].astype(jnp.float32).reshape(1, feat)
    i_in.wait()
    for cp in h_in:
        cp.wait()
    pl.semaphore_wait(barrier, n - 1)

    def hop(src, leg, q, peer):
        return remote(gath.at[src, q], h_send.at[leg, q], h_recv.at[leg, q], peer)

    def to_mate(src, leg, q):
        return remote(gath.at[src, q], mate_send.at[leg, q], mate_recv.at[leg, q], mate)

    s_copies = [remote(s_all.at[me], s_send.at[d - 1], s_recv.at[d - 1], lax.rem(me + d, n)) for d in range(1, n)]
    sent = []

    def send(cp):
        cp.start()
        sent.append(cp)

    for q in range(halves):
        send(hop(me, 0, q, onward))
        send(hop(me, 1, q, behind))
    for cp in s_copies:
        send(cp)
    for q in range(halves):
        send(to_mate(me, 0, q))

    def squares(d):
        h32 = gath[d].astype(jnp.float32)
        h2 = jnp.sum((h32 * h32).reshape(halves, feat // 8, 8, 128), axis=1)
        for q in range(halves):
            sq_part[d, :, q * 128:(q + 1) * 128] = h2[q]

    for q in range(halves):
        hop(behind, 0, q, onward).wait_recv()
        send(hop(behind, 2, q, onward))
        send(to_mate(behind, 1, q))
        hop(onward, 1, q, behind).wait_recv()
        send(to_mate(onward, 2, q))
    squares(me)
    squares(behind)
    squares(onward)
    for cp in s_copies:
        cp.wait_recv()
    for d in range(n):
        pad = jnp.zeros((1, 256 - feat), jnp.float32)
        s_wide = jnp.broadcast_to(jnp.concatenate([1.0 + s_all[d], pad], axis=1), (128, 256))
        s_col[d * feat:(d + 1) * feat, :] = s_wide.T[:feat, :]
    for leg, src in ((0, mate), (1, onward + 1 - 2 * core), (2, behind + 1 - 2 * core)):
        for q in range(halves):
            to_mate(src, leg, q).wait_recv()
    for d in (0, 2, n - 2):
        squares(lax.rem(mate + d, n))
    for q in range(halves):
        hop(across, 2, q, onward).wait_recv()
        send(to_mate(across, 3, q))
    squares(across)
    far = lax.rem(mate + 4, n)
    for q in range(halves):
        to_mate(far, 3, q).wait_recv()
    squares(far)

    sq = sq_part[0]
    for d in range(1, n):
        sq = sq + sq_part[d]
    inv = lax.rsqrt(jnp.sum(sq, axis=0, keepdims=True) / width + NORM_EPS)
    for d in range(n):
        scale = s_col[d * feat:(d + 1) * feat, :]
        for q in range(halves):
            cols = slice(q * 128, (q + 1) * 128)
            normed[d * feat:(d + 1) * feat, cols] = (gath[d, q].astype(jnp.float32) * inv[:, cols] * scale).astype(jnp.bfloat16)
    for cp in sent:
        cp.wait_send()

    def multiply(j, z_ref):
        z_ref[...] = jnp.dot(ebuf[lax.rem(j, RING)], normed[...], preferred_element_type=jnp.float32)

    first = me * vocab
    sub = lax.broadcasted_iota(jnp.int32, (8, rows), 0)

    def finish(j, z_ref, carry):
        acc, picks = carry[0], list(carry[1:])
        want = [ids_ref[k:k + 1, :] - (first + j * CHUNK) - sub for k in range(n_cand)]
        for b in range(CHUNK // 128):
            x = z_ref[b * 128:(b + 1) * 128, :]
            t = jnp.tanh(x * (1.0 / SOFT_CAP))
            e = jnp.exp2(t * (SOFT_CAP * LOG2E))
            acc = acc + jnp.sum(e.reshape(16, 8, rows), axis=0)
            c = t * SOFT_CAP
            for g in range(16):
                part = c[g * 8:(g + 1) * 8, :]
                for k in range(n_cand):
                    picks[k] = jnp.where(want[k] == b * 128 + g * 8, part, picks[k])
            c_ref[:, pl.ds(pl.multiple_of(j * CHUNK + b * 128, 128), 128)] = c.T
        return (acc, *picks)

    table_copy(0).wait()
    multiply(0, z_a)

    def pair(p, acc):
        a = 2 * p
        for k in (1, 2):
            table_copy(a + k).wait()
        for k in (-1, 0):
            nxt = a + k + RING

            @pl.when((nxt >= RING) & (nxt < n_chunks))
            def _():
                table_copy(nxt).start()
        multiply(a + 1, z_b)
        acc = finish(a, z_a, acc)
        multiply(a + 2, z_a)
        return finish(a + 1, z_b, acc)

    acc = lax.fori_loop(0, n_chunks // 2 - 1, pair, (jnp.zeros((8, rows), jnp.float32),) * (1 + n_cand))
    table_copy(n_chunks - 1).wait()
    multiply(n_chunks - 1, z_b)
    acc = finish(n_chunks - 2, z_a, acc)
    acc = finish(n_chunks - 1, z_b, acc)

    for k, part in enumerate(acc):
        stats[me, k:k + 1, :] = jnp.sum(part, axis=0, keepdims=True)
    st_copies = [remote(stats.at[me], st_send.at[d - 1], st_recv.at[d - 1], lax.rem(me + d, n)) for d in range(1, n)]
    for cp in st_copies:
        cp.start()
    for cp in st_copies:
        cp.wait()
    total = stats[0]
    for d in range(1, n):
        total = total + stats[d]
    lse = jnp.log(total[0:1, :])
    tail_ref[0:1, :] = lse
    tail_ref[1:1 + n_cand, :] = total[1:1 + n_cand, :] - lse


def write_kernel(c_ref, tail_ref, lse_hbm, cand_hbm, out_hbm, lse_buf, cand_buf, l_col, obuf, o_sem, t_sem):
    rows, vocab = c_ref.shape
    lse_buf[...] = tail_ref[0:1, :]
    cand_buf[...] = tail_ref[1:1 + cand_buf.shape[0], :]
    for b in range(rows // 128):
        l_col[b * 128:(b + 1) * 128, :] = jnp.broadcast_to(tail_ref[0:1, b * 128:(b + 1) * 128], (128, 128)).T
    small = [pltpu.make_async_copy(lse_buf, lse_hbm, t_sem.at[0]), pltpu.make_async_copy(cand_buf, cand_hbm, t_sem.at[1])]
    for cp in small:
        cp.start()
    n_blk = rows // OUT_ROWS

    def out_copy(i, slot):
        return pltpu.make_async_copy(
            obuf.at[slot], out_hbm.at[pl.ds(pl.multiple_of(i * OUT_ROWS, OUT_ROWS), OUT_ROWS), :], o_sem.at[slot])

    def block(i, carry):
        slot = lax.rem(i, OUT_RING)

        @pl.when(i >= OUT_RING)
        def _():
            out_copy(i - OUT_RING, slot).wait()
        r0 = pl.multiple_of(i * OUT_ROWS, OUT_ROWS)
        col = l_col[pl.ds(r0, OUT_ROWS), :]
        step = 2048

        def part(q, c):
            v0 = pl.multiple_of(q * step, step)
            lse = jnp.concatenate([col] * (step // 128), axis=1)
            obuf[slot, :, pl.ds(v0, step)] = (c_ref[pl.ds(r0, OUT_ROWS), pl.ds(v0, step)] - lse).astype(jnp.bfloat16)
            return c

        lax.fori_loop(0, vocab // step, part, 0)
        out_copy(i, slot).start()
        return carry

    lax.fori_loop(0, n_blk, block, 0)
    for i in range(n_blk - OUT_RING, n_blk):
        out_copy(i, i % OUT_RING).wait()
    for cp in small:
        cp.wait()


def solution(mesh):
    n = mesh.shape["tp"]

    def device_step(hidden_blk, cand_ids, scale_blk, table_blk):
        rows, feat = hidden_blk.shape
        vocab, width = table_blk.shape
        n_cand = cand_ids.shape[1]
        ids_t = cand_ids.T
        dma = pltpu.SemaphoreType.DMA
        any_space = pl.BlockSpec(memory_space=pl.ANY)
        vmem = pl.BlockSpec(memory_space=pltpu.VMEM)
        capped, tail = pl.pallas_call(
            functools.partial(head_kernel, n),
            out_shape=(pltpu.VMEM((rows, vocab), jnp.float32),
                       pltpu.VMEM((8, rows), jnp.float32)),
            in_specs=[any_space] * 4,
            out_specs=(vmem, vmem),
            scratch_shapes=[
                pltpu.VMEM((RING, CHUNK, width), jnp.bfloat16),
                pltpu.VMEM((n, rows // 128, feat, 128), jnp.bfloat16),
                pltpu.VMEM((feat,), jnp.bfloat16),
                pltpu.VMEM((n, 1, feat), jnp.float32),
                pltpu.VMEM((n * feat, 128), jnp.float32),
                pltpu.VMEM((n, 8, rows), jnp.float32),
                pltpu.VMEM((n * feat, rows), jnp.bfloat16),
                pltpu.VMEM((CHUNK, rows), jnp.float32),
                pltpu.VMEM((CHUNK, rows), jnp.float32),
                pltpu.VMEM((n_cand, rows), jnp.int32),
                pltpu.VMEM((n, 8, rows), jnp.float32),
                dma((RING,)), dma((rows // 128 + 2,)), dma((n - 1,)), dma((n - 1,)),
                dma((3, rows // 128)), dma((3, rows // 128)), dma((4, rows // 128)), dma((4, rows // 128)),
                dma((n - 1,)), dma((n - 1,)),
            ],
            compiler_params=pltpu.CompilerParams(
                collective_id=0, has_side_effects=True, vmem_limit_bytes=31 * 2**20),
        )(hidden_blk.T, scale_blk, ids_t, table_blk)
        lse, cand, logp = pl.pallas_call(
            write_kernel,
            out_shape=(jax.ShapeDtypeStruct((1, rows), jnp.float32),
                       jax.ShapeDtypeStruct((n_cand, rows), jnp.float32),
                       jax.ShapeDtypeStruct((rows, vocab), jnp.bfloat16)),
            in_specs=[vmem, vmem],
            out_specs=(any_space,) * 3,
            scratch_shapes=[pltpu.VMEM((1, rows), jnp.float32),
                            pltpu.VMEM((n_cand, rows), jnp.float32),
                            pltpu.VMEM((rows, 128), jnp.float32),
                            pltpu.VMEM((OUT_RING, OUT_ROWS, vocab), jnp.bfloat16),
                            dma((OUT_RING,)), dma((2,))],
            compiler_params=pltpu.CompilerParams(vmem_limit_bytes=31 * 2**20),
        )(pltpu.with_memory_space_constraint(capped, pltpu.VMEM),
          pltpu.with_memory_space_constraint(tail, pltpu.VMEM))
        return lse.reshape(rows), cand.T, logp

    return jax.shard_map(
        device_step,
        mesh=mesh,
        in_specs=(P("dp", "tp"), P("dp", None), P("tp"), P("tp", None)),
        out_specs=(P("dp"), P("dp", None), P("dp", "tp")),
        check_vma=False,
    )
```

time: 58.6 us -> 55.7 us (0.951)
  Pallas kernels: 56.6 us -> 54.9 us
  local copies, waits for them, and re-layouts: 1.22 us -> 0 us
    pallas_call x1, Pallas kernels: 7.46 us -> 6.18 us  [device_step(): pl.pallas_call(write_kernel, out_shape=(jax.ShapeDtypeStruct((1, rows), j...]
    reshape x1 -> x0, local copies, waits for them, and re-layouts: 1.22 us -> none  [device_step(): scale_blk.reshape(1, feat)]
where the time goes in v2:
time: 55.7 us; the launch traced here: 55.6 us
  Pallas kernels  54.9 us (99%)
  between operations  0.64 us (1%)
    pallas_call x1, Pallas kernels, device_step(): pl.pallas_call(functools.partial(head_kernel, n), out_shape=(pltpu.VMEM((...  48.8 us
    pallas_call x1, Pallas kernels, device_step(): pl.pallas_call(write_kernel, out_shape=(jax.ShapeDtypeStruct((1, rows), j...  6.18 us

profile of v2, /device:TPU:113, one launch (start us, length us, event | category | flops | bytes accessed | tf_op | source)
XLA Modules:
  0.0 55.6 jit_solution(3401455188834715779)
XLA Ops:
  0.6 48.8 %shard_map.67 = (f32[256,32768]{1,0:T(8,128)S(1)}, f32[8,256]{1,0:T(8,128)S(1)}) custom-call(bf16[144,256]{1,0:T(8,128)(2,1)} %bitcast.4, bf16[144]{0:T(256)(128)(2,1)} %s_hbm.1, s32[4,256]{1,0:T(4,128)} %bitcast.5, bf16[32768,1152]{1,0:T(8,128)(2,1)} %tab_hbm.1), custom_call_target="tpu_custom_call" | custom-call | tf_op jit(solution)/shard_map/pallas_call | solution.py:247
  49.4 6.2 %shard_map.68 = (f32[1,256]{1,0:T(1,128)}, f32[4,256]{1,0:T(4,128)}, bf16[256,32768]{1,0:T(8,128)(2,1)}) custom-call(f32[256,32768]{1,0:T(8,128)S(1)} %get-tuple-element.8.c_ref, f32[8,256]{1,0:T(8,128)S(1)} %get-tuple-element.9.tail_ref), custom_call_target="tpu_custom_call" | custom-call | tf_op jit(solution)/shard_map/pallas_call | solution.py:272

commit v3 on v2

--- a/solution.py
+++ b/solution.py
@@ -18,8 +18,8 @@
 MESH = pl.DeviceIdType.MESH
 
 
-def head_kernel(n, h_hbm, s_hbm, ids_hbm, tab_hbm, c_ref, tail_ref,
-                ebuf, gath, s_own, s_all, s_col, sq_part, normed, z_a, z_b, ids_ref, stats,
+def head_kernel(n, h_hbm, s_hbm, ids_hbm, tab_hbm, t_ref, tail_ref,
+                ebuf, gath, s_own, s_all, s_col, sq_part, normed, z_a, z_b, ids_sm, ids_ref, ids_blk, picked, stats,
                 e_sem, in_sem, s_send, s_recv, h_send, h_recv, mate_send, mate_recv, st_send, st_recv):
     me = lax.axis_index("tp")
     core = lax.rem(me, 2)
@@ -51,6 +51,7 @@
     for cp in h_in + [s_in, i_in]:
         cp.start()
     barrier = pltpu.get_barrier_semaphore()
+    first = me * vocab
     for d in range(1, n):
         pl.semaphore_signal(barrier, inc=1, device_id={"tp": lax.rem(me + d, n)}, device_id_type=MESH)
     for j in range(RING):
@@ -95,6 +96,8 @@
         send(to_mate(behind, 1, q))
         hop(onward, 1, q, behind).wait_recv()
         send(to_mate(onward, 2, q))
+    block_of = lax.max(lax.min(lax.shift_right_arithmetic(ids_ref[...] - first, 7), vocab // 128 - 1), 0)
+    ids_blk[...] = block_of
     squares(me)
     squares(behind)
     squares(onward)
@@ -127,30 +130,19 @@
         for q in range(halves):
             cols = slice(q * 128, (q + 1) * 128)
             normed[d * feat:(d + 1) * feat, cols] = (gath[d, q].astype(jnp.float32) * inv[:, cols] * scale).astype(jnp.bfloat16)
-    for cp in sent:
-        cp.wait_send()
+    to_smem = pltpu.make_async_copy(ids_blk, ids_sm, in_sem.at[halves + 2])
+    to_smem.start()
 
     def multiply(j, z_ref):
         z_ref[...] = jnp.dot(ebuf[lax.rem(j, RING)], normed[...], preferred_element_type=jnp.float32)
 
-    first = me * vocab
-    sub = lax.broadcasted_iota(jnp.int32, (8, rows), 0)
-
-    def finish(j, z_ref, carry):
-        acc, picks = carry[0], list(carry[1:])
-        want = [ids_ref[k:k + 1, :] - (first + j * CHUNK) - sub for k in range(n_cand)]
+    def finish(j, z_ref, acc):
         for b in range(CHUNK // 128):
-            x = z_ref[b * 128:(b + 1) * 128, :]
-            t = jnp.tanh(x * (1.0 / SOFT_CAP))
+            t = jnp.tanh(z_ref[b * 128:(b + 1) * 128, :] * (1.0 / SOFT_CAP))
             e = jnp.exp2(t * (SOFT_CAP * LOG2E))
             acc = acc + jnp.sum(e.reshape(16, 8, rows), axis=0)
-            c = t * SOFT_CAP
-            for g in range(16):
-                part = c[g * 8:(g + 1) * 8, :]
-                for k in range(n_cand):
-                    picks[k] = jnp.where(want[k] == b * 128 + g * 8, part, picks[k])
-            c_ref[:, pl.ds(pl.multiple_of(j * CHUNK + b * 128, 128), 128)] = c.T
-        return (acc, *picks)
+            t_ref[j * (CHUNK // 128) + b] = t.T.reshape(rows // 8, 8, 128)
+        return acc
 
     table_copy(0).wait()
     multiply(0, z_a)
@@ -170,29 +162,48 @@
         multiply(a + 2, z_a)
         return finish(a + 1, z_b, acc)
 
-    acc = lax.fori_loop(0, n_chunks // 2 - 1, pair, (jnp.zeros((8, rows), jnp.float32),) * (1 + n_cand))
+    acc = lax.fori_loop(0, n_chunks // 2 - 1, pair, jnp.zeros((8, rows), jnp.float32))
     table_copy(n_chunks - 1).wait()
     multiply(n_chunks - 1, z_b)
     acc = finish(n_chunks - 2, z_a, acc)
     acc = finish(n_chunks - 1, z_b, acc)
 
-    for k, part in enumerate(acc):
-        stats[me, k:k + 1, :] = jnp.sum(part, axis=0, keepdims=True)
+    stats[me, 0:1, :] = jnp.sum(acc, axis=0, keepdims=True)
+    sub = lax.broadcasted_iota(jnp.int32, (8, 128), 0)
+
+    to_smem.wait()
+
+    def pick(g, carry):
+        for k in range(n_cand):
+            tile = jnp.zeros((8, 128), jnp.float32)
+            for r in range(8):
+                tile = jnp.where(sub == r, t_ref[ids_sm[k, g * 8 + r], g], tile)
+            picked[k, g] = tile
+        return carry
+
+    lax.fori_loop(0, rows // 8, pick, 0)
+    lane = lax.broadcasted_iota(jnp.int32, (128, rows), 0)
+    for k in range(n_cand):
+        loc = ids_ref[k:k + 1, :] - first
+        hit = (lane == lax.rem(loc, 128)) & (loc >= 0) & (loc < vocab)
+        stats[me, 1 + k:2 + k, :] = jnp.sum(jnp.where(hit, picked[k].reshape(rows, 128).T, 0.0), axis=0, keepdims=True)
     st_copies = [remote(stats.at[me], st_send.at[d - 1], st_recv.at[d - 1], lax.rem(me + d, n)) for d in range(1, n)]
     for cp in st_copies:
         cp.start()
     for cp in st_copies:
         cp.wait()
+    for cp in sent:
+        cp.wait_send()
     total = stats[0]
     for d in range(1, n):
         total = total + stats[d]
     lse = jnp.log(total[0:1, :])
     tail_ref[0:1, :] = lse
-    tail_ref[1:1 + n_cand, :] = total[1:1 + n_cand, :] - lse
-
-
-def write_kernel(c_ref, tail_ref, lse_hbm, cand_hbm, out_hbm, lse_buf, cand_buf, l_col, obuf, o_sem, t_sem):
-    rows, vocab = c_ref.shape
+    tail_ref[1:1 + n_cand, :] = total[1:1 + n_cand, :] * SOFT_CAP - lse
+
+
+def write_kernel(t_ref, tail_ref, lse_hbm, cand_hbm, out_hbm, lse_buf, cand_buf, l_col, obuf, o_sem, t_sem):
+    rows, vocab = out_hbm.shape
     lse_buf[...] = tail_ref[0:1, :]
     cand_buf[...] = tail_ref[1:1 + cand_buf.shape[0], :]
     for b in range(rows // 128):
@@ -214,15 +225,15 @@
             out_copy(i - OUT_RING, slot).wait()
         r0 = pl.multiple_of(i * OUT_ROWS, OUT_ROWS)
         col = l_col[pl.ds(r0, OUT_ROWS), :]
-        step = 2048
+        tiles = 16
 
         def part(q, c):
-            v0 = pl.multiple_of(q * step, step)
-            lse = jnp.concatenate([col] * (step // 128), axis=1)
-            obuf[slot, :, pl.ds(v0, step)] = (c_ref[pl.ds(r0, OUT_ROWS), pl.ds(v0, step)] - lse).astype(jnp.bfloat16)
+            for v in range(tiles):
+                t = t_ref[q * tiles + v, pl.ds(i * (OUT_ROWS // 8), OUT_ROWS // 8)].reshape(OUT_ROWS, 128)
+                obuf[slot, :, pl.ds(pl.multiple_of(q * (tiles * 128) + v * 128, 128), 128)] = (t * SOFT_CAP - col).astype(jnp.bfloat16)
             return c
 
-        lax.fori_loop(0, vocab // step, part, 0)
+        lax.fori_loop(0, vocab // (128 * tiles), part, 0)
         out_copy(i, slot).start()
         return carry
 
@@ -246,7 +257,7 @@
         vmem = pl.BlockSpec(memory_space=pltpu.VMEM)
         capped, tail = pl.pallas_call(
             functools.partial(head_kernel, n),
-            out_shape=(pltpu.VMEM((rows, vocab), jnp.float32),
+            out_shape=(pltpu.VMEM((vocab // 128, rows // 8, 8, 128), jnp.float32),
                        pltpu.VMEM((8, rows), jnp.float32)),
             in_specs=[any_space] * 4,
             out_specs=(vmem, vmem),
@@ -260,9 +271,12 @@
                 pltpu.VMEM((n * feat, rows), jnp.bfloat16),
                 pltpu.VMEM((CHUNK, rows), jnp.float32),
                 pltpu.VMEM((CHUNK, rows), jnp.float32),
+                pltpu.SMEM((n_cand, rows), jnp.int32),
                 pltpu.VMEM((n_cand, rows), jnp.int32),
+                pltpu.VMEM((n_cand, rows), jnp.int32),
+                pltpu.VMEM((n_cand, rows // 8, 8, 128), jnp.float32),
                 pltpu.VMEM((n, 8, rows), jnp.float32),
-                dma((RING,)), dma((rows // 128 + 2,)), dma((n - 1,)), dma((n - 1,)),
+                dma((RING,)), dma((rows // 128 + 3,)), dma((n - 1,)), dma((n - 1,)),
                 dma((3, rows // 128)), dma((3, rows // 128)), dma((4, rows // 128)), dma((4, rows // 128)),
                 dma((n - 1,)), dma((n - 1,)),
             ],

time: 55.7 us -> 54.5 us (0.978)
  Pallas kernels: 54.9 us -> 53.8 us
    pallas_call x1, Pallas kernels: 48.8 us -> 45.4 us  [device_step(): pl.pallas_call(functools.partial(head_kernel, n), out_shape=(pltpu.VMEM((...]
    pallas_call x1, Pallas kernels: 6.18 us -> 8.39 us  [device_step(): pl.pallas_call(write_kernel, out_shape=(jax.ShapeDtypeStruct((1, rows), j...]
where the time goes in v3:
time: 54.5 us
  Pallas kernels  53.8 us (99%)
  between operations  0.64 us (1%)
    pallas_call x1, Pallas kernels, device_step(): pl.pallas_call(functools.partial(head_kernel, n), out_shape=(pltpu.VMEM((...  45.4 us
    pallas_call x1, Pallas kernels, device_step(): pl.pallas_call(write_kernel, out_shape=(jax.ShapeDtypeStruct((1, rows), j...  8.39 us

profile of v3, /device:TPU:113, one launch (start us, length us, event | category | flops | bytes accessed | tf_op | source)
XLA Modules:
  0.0 54.5 jit_solution(721222660132347704)
XLA Ops:
  0.6 45.4 %shard_map.67 = (f32[256,32,8,128]{3,2,1,0:T(8,128)S(1)}, f32[8,256]{1,0:T(8,128)S(1)}) custom-call(bf16[144,256]{1,0:T(8,128)(2,1)} %bitcast.4, bf16[144]{0:T(256)(128)(2,1)} %s_hbm.1, s32[4,256]{1,0:T(4,128)} %bitcast.5, bf16[32768,1152]{1,0:T(8,128)(2,1)} %tab_hbm.1), custom_call_target="tpu_custom_call" | custom-call | tf_op jit(solution)/shard_map/pallas_call | solution.py:258
  46.1 8.4 %shard_map.68 = (f32[1,256]{1,0:T(1,128)}, f32[4,256]{1,0:T(4,128)}, bf16[256,32768]{1,0:T(8,128)(2,1)}) custom-call(f32[256,32,8,128]{3,2,1,0:T(8,128)S(1)} %get-tuple-element.8.t_ref, f32[8,256]{1,0:T(8,128)S(1)} %get-tuple-element.9.tail_ref), custom_call_target="tpu_custom_call" | custom-call | tf_op jit(solution)/shard_map/pallas_call | solution.py:286
